TPU v7x, 32 devices: a 4x4x1 block of a 4x4x8 slice. The times are simulated.
32 devices in a mesh: data: 1 (over z), node: 4 (over y), expert: 8 (over x, core).
Axes of the slice: x: 4, y: 4, z: 1, core: 2. Of those that a mesh axis runs over, the one named last changes fastest.
The devices are a block of a 4x4x8 slice.
Arguments:
- tokens: bfloat16 [32768, 768], P(('data', 'node', 'expert'))
- expert_ids: int32 [32768, 1], P(('data', 'node', 'expert'))
- gate_weights: float32 [32768, 1], P(('data', 'node', 'expert'))
- slot_ids: int32 [32768, 1], P(('data', 'node', 'expert'))
- w_gate: bfloat16 [32, 768, 3072], P(('node', 'expert'))
- w_up: bfloat16 [32, 768, 3072], P(('node', 'expert'))
- w_down: bfloat16 [32, 3072, 768], P(('node', 'expert'))
Outputs:
- output: bfloat16 [32768, 768], P(('data', 'node', 'expert'))
All inputs are finite; a program needn't handle non-finite values.
Results may differ from a plain program's by a relative error of at most 0.001.
Values are sent between devices in bfloat16 or wider.
A program may use at most 768 MiB of HBM per device.

v0:
```python
import jax
import jax.numpy as jnp
from jax import lax
from jax.sharding import PartitionSpec as P

CAP_FACTOR = 2


def capacity(rows, top_k, experts):
    return ((CAP_FACTOR * rows * top_k + 8 * experts - 1) // (8 * experts)) * 8


def solution(mesh):
    group_axes = ("node", "expert")
    group_size = mesh.shape["node"] * mesh.shape["expert"]
    tok_spec = P(("data", "node", "expert"), None)
    weight_spec = P(("node", "expert"), None, None)

    def local_layer(tokens, expert_ids, gate_weights, slot_ids, w_gate, w_up, w_down):
        rows, width = tokens.shape
        top_k = expert_ids.shape[1]
        local_experts = w_gate.shape[0]
        experts = local_experts * group_size
        slot_count = capacity(rows, top_k, experts)
        flat_pos = jnp.where(slot_ids >= 0, expert_ids * slot_count + slot_ids, experts * slot_count)
        tok_index = jnp.broadcast_to(jnp.arange(rows, dtype=jnp.int32)[:, None], (rows, top_k))
        src_table = jnp.full((experts * slot_count,), rows, jnp.int32).at[flat_pos.reshape(-1)].set(tok_index.reshape(-1), mode="drop")
        send_buf = jnp.take(tokens, src_table, axis=0, mode="fill", fill_value=0)
        send_buf = send_buf.reshape(group_size, local_experts, 1, slot_count, width)
        recv_buf = lax.all_to_all(send_buf, group_axes, 0, 2, tiled=True)
        recv_buf = recv_buf.reshape(local_experts, group_size * slot_count, width)
        proj_gate = jnp.einsum("erd,edf->erf", recv_buf, w_gate, preferred_element_type=jnp.float32)
        proj_up = jnp.einsum("erd,edf->erf", recv_buf, w_up, preferred_element_type=jnp.float32)
        hidden = (jax.nn.silu(proj_gate) * proj_up).astype(jnp.bfloat16)
        expert_out = jnp.einsum("erf,efd->erd", hidden, w_down, preferred_element_type=jnp.float32).astype(jnp.bfloat16)
        expert_out = expert_out.reshape(local_experts, group_size, slot_count, width)
        returned = lax.all_to_all(expert_out, group_axes, 1, 0, tiled=True)
        returned = returned.reshape(experts * slot_count, width)
        picked = jnp.take(returned, flat_pos, axis=0, mode="fill", fill_value=0)
        combined = jnp.sum(gate_weights[:, :, None] * picked.astype(jnp.float32), axis=1)
        return combined.astype(jnp.bfloat16)

    return jax.shard_map(local_layer, mesh=mesh, in_specs=(tok_spec, tok_spec, tok_spec, tok_spec, weight_spec, weight_spec, weight_spec), out_specs=tok_spec, check_vma=False)
```

profile of v0, /device:TPU:96, one launch (start us, length us, event | category | flops | bytes accessed | tf_op | source)
XLA Modules:
  0.0 163.3 jit_solution(11545370428002738694)
XLA Ops:
  0.0 0.0 copy-start
  0.0 0.9 and_reduce_fusion
  0.9 4.3 %scatter_custom_fusion = s32[2048]{0:T(1024)S(1)} fusion(s32[1024]{0:T(1024)S(1)} %bitcast.31, s32[1024]{0:T(1024)S(1)} %iota.3, s32[]{:T(128)} %constant.24.clone.1), kind=kCustom, calls=%fused_computation.18 | custom fusion | bytes 8196 | tf_op jit(solution)/shard_map/scatter | solution.py:27
  5.2 0.1 broadcast_in_dim.41
  5.3 0.0 copy-done
  5.3 9.4 %gather_fusion = bf16[2048,768]{1,0:T(8,128)(2,1)} fusion(bf16[1024,768]{1,0:T(8,128)(2,1)S(1)} %copy-done, s32[2048]{0:T(1024)S(1)} %fusion.11), kind=kCustom, calls=%fused_computation | custom fusion | bytes 6299648 | tf_op jit(solution)/shard_map/jit(_take)/gather | solution.py:28
  14.7 2.1 %broadcast_select_fusion = bf16[32,1,1,64,768]{4,3,2,1,0:T(8,128)(2,1)S(1)} fusion(bf16[32,1,1,64,768]{4,3,2,1,0:T(8,128)(2,1)} %bitcast.27, pred[32,64]{1,0:T(8,128)(4,1)S(1)} %broadcast_in_dim.41), kind=kLoop, calls=%fused_computation.11 | loop fusion | flops 1572864 | bytes 6293504 | tf_op jit(solution)/shard_map/jit(_take)/select_n | solution.py:28
  16.8 0.0 copy-start.3
  16.8 47.9 %all_to_all.8 = bf16[32,1,1,64,768]{4,3,2,1,0:T(8,128)(2,1)S(1)} all-to-all(bf16[32,1,1,64,768]{4,3,2,1,0:T(8,128)(2,1)S(1)} %broadcast_select_fusion), channel_id=1, replica_groups=mesh['data'=1,'node'=4,'expert'=8] {'node','expert'}, dimensions={0} | all-to-all | bytes 6291456 | tf_op jit(solution)/shard_map/all_to_all | solution.py:30
  64.7 0.0 copy-start.1
  64.7 1.7 %copy-done.1 = bf16[32,1,1,64,768]{4,3,2,1,0:T(8,128)(2,1)} copy-done((bf16[32,1,1,64,768]{4,3,2,1,0:T(8,128)(2,1)}, bf16[32,1,1,64,768]{4,3,2,1,0:T(8,128)(2,1)S(1)}, u32[]{:S(2)}) %copy-start.1) | copy-done | bytes 3145752
  66.5 0.0 copy-done.3
  66.5 13.3 %fusion.4 = f32[2048,3072]{1,0:T(8,128)} fusion(bf16[2048,768]{1,0:T(8,128)(2,1)S(1)} %bitcast.29, bf16[1,768,3072]{2,1,0:T(8,128)(2,1)S(1)} %copy-done.3), kind=kOutput, calls=%fused_computation.7 | convolution fusion | flops 9663676416 | bytes 33030144 | tf_op jit(solution)/shard_map/erd,edf->erf/dot_general | solution.py:32
  79.7 28.4 %fusion.6 = bf16[2048,768]{1,0:T(8,128)(2,1)} fusion(bf16[1,3072,768]{2,1,0:T(8,128)(2,1)} %param.13, f32[2048,3072]{1,0:T(8,128)} %fusion.4, bf16[2048,768]{1,0:T(8,128)(2,1)} %bitcast.30, bf16[1,768,3072]{2,1,0:T(8,128)(2,1)} %param.12), kind=kOutput, calls=%fused_computation.9 | convolution fusion | flops 19366674432 | bytes 40894464 | tf_op jit(solution)/shard_map/erf,efd->erd/dot_general | solution.py:35
  108.1 5.2 %all-to-all-start.1 = ((bf16[1,32,64,768]{3,2,0,1:T(8,128)(2,1)}), bf16[1,32,64,768]{3,2,0,1:T(8,128)(2,1)}, u32[]{:S(2)}, u32[]{:S(2)}) async-start(bf16[1,32,64,768]{3,2,0,1:T(8,128)(2,1)} %bitcast.28), calls=%async_computation.1 | async-start | bytes 6291456 | tf_op jit(solution)/shard_map/all_to_all | solution.py:37
  113.3 41.6 %all-to-all-done.1 = bf16[1,32,64,768]{3,2,0,1:T(8,128)(2,1)} async-done(((bf16[1,32,64,768]{3,2,0,1:T(8,128)(2,1)}), bf16[1,32,64,768]{3,2,0,1:T(8,128)(2,1)}, u32[]{:S(2)}, u32[]{:S(2)}) %all-to-all-start.1) | async-done | bytes 3145760 | tf_op jit(solution)/shard_map/all_to_all | solution.py:37
  154.9 0.0 copy-start.2
  154.9 6.8 %gather_fusion.1 = bf16[1024,768]{1,0:T(8,128)(2,1)S(1)} fusion(bf16[2048,768]{1,0:T(8,128)(2,1)} %bitcast.10, s32[1024]{0:T(1024)S(1)} %broadcast_clamp_fusion), kind=kCustom, calls=%fused_computation.1 | custom fusion | bytes 3149824 | tf_op jit(solution)/shard_map/jit(_take)/gather | solution.py:39
  161.7 0.0 copy-done.2
  161.7 1.6 multiply_convert_fusion.1
  (4 shorter events, 0.0 us)
Async XLA Ops:
  0.0 5.3 %copy-start = (bf16[1024,768]{1,0:T(8,128)(2,1)S(1)}, bf16[1024,768]{1,0:T(8,128)(2,1)}, u32[]{:S(2)}) copy-start(bf16[1024,768]{1,0:T(8,128)(2,1)} %param.7) | copy-start | bytes 4718596
  16.8 49.6 %copy-start.3 = (bf16[1,768,3072]{2,1,0:T(8,128)(2,1)S(1)}, bf16[1,768,3072]{2,1,0:T(8,128)(2,1)}, u32[]{:S(2)}) copy-start(bf16[1,768,3072]{2,1,0:T(8,128)(2,1)} %param.11) | copy-start | bytes 14155780
  64.7 1.7 %copy-start.1 = (bf16[32,1,1,64,768]{4,3,2,1,0:T(8,128)(2,1)}, bf16[32,1,1,64,768]{4,3,2,1,0:T(8,128)(2,1)S(1)}, u32[]{:S(2)}) copy-start(bf16[32,1,1,64,768]{4,3,2,1,0:T(8,128)(2,1)S(1)} %all_to_all.8) | copy-start | bytes 9437188
  108.1 46.8 %all-to-all-start.1 = ((bf16[1,32,64,768]{3,2,0,1:T(8,128)(2,1)}), bf16[1,32,64,768]{3,2,0,1:T(8,128)(2,1)}, u32[]{:S(2)}, u32[]{:S(2)}) async-start(bf16[1,32,64,768]{3,2,0,1:T(8,128)(2,1)} %bitcast.28), calls=%async_computation.1 | async-start | bytes 6291456 | tf_op jit(solution)/shard_map/all_to_all | solution.py:37
  154.9 6.8 %copy-start.2 = (f32[1024,1]{0,1:T(1,128)S(1)}, f32[1024,1]{0,1:T(1,128)}, u32[]{:S(2)}) copy-start(f32[1024,1]{0,1:T(1,128)} %param.9) | copy-start | bytes 12292
where the time goes:
time: 164 us; the launch traced here: 163 us
  blocking collectives  47.9 us (29%)
  matrix products  41.6 us (25%)
  waiting for transfers between devices  41.6 us (25%)
  local copies, waits for them, and re-layouts  22.3 us (14%)
  starting transfers between devices  5.18 us (3%)
  other arithmetic  4.57 us (3%)
    all_to_all x1, blocking collectives, local_layer(): recv_buf = lax.all_to_all(send_buf, group_axes, 0, 2, tiled=True)  47.9 us
    all_to_all x1, waiting for transfers between devices, local_layer(): returned = lax.all_to_all(expert_out, group_axes, 1, 0, tiled=True)  41.6 us
    dot_general x1, matrix products, local_layer(): jnp.einsum('erf,efd->erd', hidden, w_down, preferred_element_type=jnp.flo...  28.4 us
    dot_general x1, matrix products, local_layer(): jnp.einsum('erd,edf->erf', recv_buf, w_gate, preferred_element_type=jnp.f...  13.3 us
    gather x1, local copies, waits for them, and re-layouts, local_layer(): send_buf = jnp.take(tokens, src_table, axis=0, mode='fill', fill_value=0)  9.42 us
    gather x1, local copies, waits for them, and re-layouts, local_layer(): picked = jnp.take(returned, flat_pos, axis=0, mode='fill', fill_value=0)  6.78 us
    all_to_all x1, starting transfers between devices, local_layer(): returned = lax.all_to_all(expert_out, group_axes, 1, 0, tiled=True)  5.18 us
    scatter x1, local copies, waits for them, and re-layouts, local_layer(): jnp.full((experts * slot_count,), rows, jnp.int32).at[flat_pos.reshape(-1)]  4.32 us
  transfers between devices with their start and end apart: 1, of which 1 were waited for; matrix products, arithmetic and copies ran while one was open for 0% of the time, Pallas kernels for 0%

commit v1 on v0

v1 whole, which is shorter than its diff:
```python
import functools
import random

import jax
import jax.numpy as jnp
from jax import lax
from jax.experimental import pallas as pl
from jax.experimental.pallas import tpu as pltpu
from jax.sharding import PartitionSpec as P

MESH = pl.DeviceIdType.MESH
CAP_FACTOR = 2
CORES = 2
F_CHUNK = 256
N_CHUNK = 256
GROUPS = (4, 4, 4, 4, 4, 4, 4, 4)


def capacity(rows, top_k, experts):
    return ((CAP_FACTOR * rows * top_k + 8 * experts - 1) // (8 * experts)) * 8


def partner_order(nodes, chips):
    offs = [(n, x, c) for n in range(nodes) for x in range(chips) for c in range(CORES)]
    rest = offs[1:]
    random.Random(10).shuffle(rest)
    return offs[:1] + rest


def group_plan(blocks):
    sizes = list(GROUPS) if sum(GROUPS) == blocks else [1] * blocks
    plan, first = [], 0
    for size in sizes:
        plan.append((first, size))
        first += size
    return plan


def kernel(order, nodes, chips, cap, ids_ref, slots_ref, gates_ref, tok_hbm, wg_hbm, wu_hbm, wd_hbm, out_ref,
           tok, wg, wu, wd, send, recv, hid, y, ret, acc, pos_b, gate_b,
           tok_sem, w_sem, s1, r1, s2, r2):
    rows, width = tok.shape
    ff = wg.shape[1]
    data, node, exp = lax.axis_index("data"), lax.axis_index("node"), lax.axis_index("expert")
    chip, core = exp // CORES, lax.rem(exp, CORES)

    def device(off, sign):
        dn, dx, dc = off
        n = lax.rem(node + (dn if sign > 0 else nodes - dn), nodes)
        x = lax.rem(chip + (dx if sign > 0 else chips - dx), chips)
        return n, x * CORES + lax.rem(core + dc, CORES)

    def expert_of(i):
        n, e = device(order[i], 1)
        return n * (chips * CORES) + e

    def block(i, size=1):
        return pl.ds(i * cap, size * cap)

    def dispatch(i):
        n, e = device(order[i], 1)
        return pltpu.make_async_remote_copy(send.at[block(i)], recv.at[block(i)], s1.at[i], r1.at[i],
                                            device_id=(data, n, e), device_id_type=MESH)

    def give_back(i):
        n, e = device(order[i], -1)
        return pltpu.make_async_remote_copy(y.at[block(i)], ret.at[block(i)], s2.at[i], r2.at[i],
                                            device_id=(data, n, e), device_id_type=MESH)

    blocks = len(order)
    plan = group_plan(blocks)

    tok_copy = pltpu.make_async_copy(tok_hbm, tok, tok_sem)
    tok_copy.start()
    w_copies = [pltpu.make_async_copy(h.at[0], v, w_sem.at[k]) for k, (h, v) in enumerate(((wg_hbm, wg), (wu_hbm, wu), (wd_hbm, wd)))]
    for c in w_copies:
        c.start()
    barrier = pltpu.get_barrier_semaphore()
    for i in range(1, blocks):
        n, e = device(order[i], 1)
        pl.semaphore_signal(barrier, inc=1, device_id=(data, n, e), device_id_type=MESH)

    ids, slots = ids_ref[...], slots_ref[...]
    pos = jnp.where(slots >= 0, ids * cap + slots, -1)
    tok_copy.wait()

    row_i = lax.broadcasted_iota(jnp.int32, (cap, rows), 0)

    def pick(first, size):
        hot = [jnp.where(pos - expert_of(i) * cap == row_i, 1.0, 0.0).astype(jnp.bfloat16) for i in range(first, first + size)]
        hot = jnp.concatenate(hot, axis=0)
        got = jnp.dot(hot, tok[...], preferred_element_type=jnp.float32).astype(jnp.bfloat16)
        if first == 0:
            recv[block(0)] = got[:cap]
        send[block(first, size)] = got

    def start_dispatch(first, size):
        for i in range(max(first, 1), first + size):
            dispatch(i).start()

    for k, (first, size) in enumerate(plan):
        pick(first, size)
        if k == 1:
            pl.semaphore_wait(barrier, blocks - 1)
        if k >= 1:
            start_dispatch(*plan[k - 1])
    start_dispatch(*plan[-1])

    lanes = 128
    for b in range(rows // lanes):
        part = pl.ds(b * lanes, lanes)
        pos_b[part, :] = jnp.transpose(jnp.broadcast_to(pos[:, b * lanes:(b + 1) * lanes], (lanes, lanes)))
        gate_b[part, :] = jnp.transpose(jnp.broadcast_to(gates_ref[:, b * lanes:(b + 1) * lanes], (lanes, lanes)))

    def expert_rows(first, size):
        m = size * cap
        x_rows = block(first, size)

        def up(f, carry):
            cols = pl.ds(pl.multiple_of(f * F_CHUNK, F_CHUNK), F_CHUNK)
            x = recv[x_rows]
            a = jnp.dot(x, wg[:, cols], preferred_element_type=jnp.float32)
            b = jnp.dot(x, wu[:, cols], preferred_element_type=jnp.float32)
            hid[pl.ds(0, m), cols] = (jax.nn.silu(a) * b).astype(jnp.bfloat16)
            return carry

        lax.fori_loop(0, ff // F_CHUNK, up, 0)

        def down(f, carry):
            cols = pl.ds(pl.multiple_of(f * N_CHUNK, N_CHUNK), N_CHUNK)
            y[x_rows, cols] = jnp.dot(hid[pl.ds(0, m), :], wd[:, cols], preferred_element_type=jnp.float32).astype(jnp.bfloat16)
            return carry

        lax.fori_loop(0, width // N_CHUNK, down, 0)

    for k, (first, size) in enumerate(plan):
        if k == 0:
            for c in w_copies:
                c.wait()
        for i in range(max(first, 1), first + size):
            dispatch(i).wait_recv()
        expert_rows(first, size)
        for i in range(max(first, 1), first + size):
            give_back(i).start()
        if first == 0:
            ret[block(0)] = y[block(0)]

    lane = lax.broadcasted_iota(jnp.int32, (1, lanes), 1)

    def picked(first, size):
        per = lanes // cap
        hots = []
        for i in range(first, first + size, per):
            want = lane + expert_of(i) * cap
            for q in range(1, per):
                want = jnp.where(lane >= q * cap, lane - q * cap + expert_of(i + q) * cap, want)
            hots.append(jnp.where(pos_b[...] == want, 1.0, 0.0).astype(jnp.bfloat16))
        hot = jnp.concatenate(hots, axis=1) if len(hots) > 1 else hots[0]
        return jnp.dot(hot, ret[block(first, size)], preferred_element_type=jnp.float32)

    for k, (first, size) in enumerate(plan):
        for i in range(max(first, 1), first + size):
            give_back(i).wait_recv()
        part = picked(first, size)
        if k == 0:
            acc[...] = part
        elif k < len(plan) - 1:
            acc[...] += part
        else:
            total = acc[...] + part
            gate = gate_b[...]
            for j in range(width // lanes):
                out_ref[:, j * lanes:(j + 1) * lanes] = (gate * total[:, j * lanes:(j + 1) * lanes]).astype(out_ref.dtype)

    for i in range(1, blocks):
        dispatch(i).wait_send()
        give_back(i).wait_send()


def solution(mesh):
    nodes, chips = mesh.shape["node"], mesh.shape["expert"] // CORES
    tok_spec = P(("data", "node", "expert"), None)
    weight_spec = P(("node", "expert"), None, None)
    order = partner_order(nodes, chips)

    def local_layer(tokens, expert_ids, gate_weights, slot_ids, w_gate, w_up, w_down):
        rows, width = tokens.shape
        ff = w_gate.shape[2]
        blocks = len(order)
        cap = capacity(rows, expert_ids.shape[1], blocks * w_gate.shape[0])
        slots = blocks * cap
        vmem, hbm = pl.BlockSpec(memory_space=pltpu.VMEM), pl.BlockSpec(memory_space=pl.ANY)
        bf16 = jnp.bfloat16
        return pl.pallas_call(
            functools.partial(kernel, order, nodes, chips, cap),
            out_shape=jax.ShapeDtypeStruct((rows, width), bf16),
            in_specs=[vmem, vmem, vmem, hbm, hbm, hbm, hbm],
            out_specs=vmem,
            scratch_shapes=[
                pltpu.VMEM((rows, width), bf16),
                pltpu.VMEM((width, ff), bf16),
                pltpu.VMEM((width, ff), bf16),
                pltpu.VMEM((ff, width), bf16),
                pltpu.VMEM((slots, width), bf16),
                pltpu.VMEM((slots, width), bf16),
                pltpu.VMEM((max(s for _, s in group_plan(blocks)) * cap, ff), bf16),
                pltpu.VMEM((slots, width), bf16),
                pltpu.VMEM((slots, width), bf16),
                pltpu.VMEM((rows, width), jnp.float32),
                pltpu.VMEM((rows, 128), jnp.int32),
                pltpu.VMEM((rows, 128), jnp.float32),
                pltpu.SemaphoreType.DMA,
                pltpu.SemaphoreType.DMA((3,)),
                pltpu.SemaphoreType.DMA((blocks,)),
                pltpu.SemaphoreType.DMA((blocks,)),
                pltpu.SemaphoreType.DMA((blocks,)),
                pltpu.SemaphoreType.DMA((blocks,)),
            ],
            compiler_params=pltpu.CompilerParams(collective_id=0, has_side_effects=True, vmem_limit_bytes=60 * 1024 * 1024),
            name="moe_exchange",
        )(expert_ids.reshape(1, rows), slot_ids.reshape(1, rows), gate_weights.reshape(1, rows), tokens, w_gate, w_up, w_down)

    return jax.shard_map(local_layer, mesh=mesh, in_specs=(tok_spec, tok_spec, tok_spec, tok_spec, weight_spec, weight_spec, weight_spec), out_specs=tok_spec, check_vma=False)
```

time: 164 us -> 93.8 us (0.57)
  the two profiles are of different devices: /device:TPU:96 before, /device:TPU:102 now
where the time goes in v1:
time: 93.8 us; the launch traced here: 93.6 us
  Pallas kernels  91 us (97%)
  local copies, waits for them, and re-layouts  2.65 us (3%)
    pallas_call x1, Pallas kernels, local_layer(): pl.pallas_call(functools.partial(kernel, order, nodes, chips, cap), out_s...  91 us
    unnamed x1, local copies, waits for them, and re-layouts  2.65 us

profile of v1, /device:TPU:102, one launch (start us, length us, event | category | flops | bytes accessed | tf_op | source)
XLA Modules:
  0.0 93.6 jit_solution(2416721419696542253)
XLA Ops:
  0.0 91.0 %moe_exchange.1 = bf16[1024,768]{1,0:T(8,128)(2,1)} custom-call(s32[1,1024]{1,0:T(1,128)} %bitcast.3, s32[1,1024]{1,0:T(1,128)} %bitcast.4, f32[1,1024]{1,0:T(1,128)} %bitcast.5, bf16[1024,768]{1,0:T(8,128)(2,1)} %tok_hbm.1, bf16[1,768,3072]{2,1,0:T(8,128)(2,1)} %wg_hbm.1, bf16[1,768,3072]{2,1,0:T(8,128)(2,1)} %wu_hbm.1, bf16[1,3072,768]{2,1,0:T(8,128)(2,1)} %wd_hbm.1), custom_call_target="tpu_custom_call" | custom-call | tf_op jit(solution)/shard_map/moe_exchange/pallas_call | solution.py:194
  91.0 2.7 %copy.9 = bf16[1024,768]{1,0:T(8,128)(2,1)} copy(bf16[1024,768]{1,0:T(8,128)(2,1)} %moe_exchange.1) | data formatting | bytes 3145728

commit v2 on v0

v2 whole, which is shorter than its diff:
```python
import functools

import jax
import jax.numpy as jnp
from jax import lax
from jax.experimental import pallas as pl
from jax.experimental.pallas import tpu as pltpu
from jax.sharding import PartitionSpec as P

MESH = pl.DeviceIdType.MESH
CAP_FACTOR = 2
CORES = 2
LANES = 128
GROUP_ROWS = 256
X, Y = 0, 1


def capacity(rows, top_k, experts):
    return ((CAP_FACTOR * rows * top_k + 8 * experts - 1) // (8 * experts)) * 8


def far_first(n):
    return sorted(range(1, n), key=lambda d: -min(d, n - d))


class Plan:
    def __init__(self, nodes, chips, cap):
        self.size = {X: chips, Y: nodes}
        self.cap, self.half = cap, cap // 2
        self.msgs = [(a, d, c) for c in range(CORES) for i in range(max(nodes, chips) - 1) for a in (X, Y)
                     for d in far_first(self.size[a])[i:i + 1]]
        self.pieces = [(m, q) for m, (a, d, c) in enumerate(self.msgs) for q in far_first(self.size[1 - a])]
        self.piece_base = (2 + len(self.msgs)) * cap
        self.rows = self.piece_base + len(self.pieces) * self.half

    def direct_rows(self, m):
        return pl.ds((2 + m) * self.cap, self.cap)

    def piece_rows(self, k):
        return pl.ds(self.piece_base + k * self.half, self.half)

    def pieces_of(self, m):
        return [k for k, (mm, _) in enumerate(self.pieces) if mm == m]

    def spans(self):
        out = [(0, self.cap, (0, 0, 0), 0), (self.cap, self.cap, (0, 0, 1), 0)]
        for m, (a, d, c) in enumerate(self.msgs):
            out.append(((2 + m) * self.cap, self.cap, (0, d, c) if a == X else (d, 0, c), 0))
        for k, (m, q) in enumerate(self.pieces):
            a, d, c = self.msgs[m]
            out.append((self.piece_base + k * self.half, self.half, (q, d, c) if a == X else (d, q, c), 0 if a == X else self.half))
        return out


def kernel(plan, ids_ref, slots_ref, tok_hbm, wg_hbm, wu_hbm, wd_hbm, out_ref,
           tok, wg, wu, wd, send, stage, recv, hid, y, stage2, ret, acc, pos_b,
           tok_sem, w_sem, s_rel, r_rel, s_dir, r_dir, s_fwd, r_fwd, s_rdir, r_rdir, s_rpc, r_rpc, s_rfw, r_rfw):
    rows = tok.shape[0]
    cap, half = plan.cap, plan.half
    nodes, chips = plan.size[Y], plan.size[X]
    data, node, exp = lax.axis_index("data"), lax.axis_index("node"), lax.axis_index("expert")
    chip, core = exp // CORES, lax.rem(exp, CORES)
    n_msgs, n_pieces = len(plan.msgs), len(plan.pieces)

    def place(dn, dx, flip):
        n, x = lax.rem(node + dn % nodes, nodes), lax.rem(chip + dx % chips, chips)
        return n, x * CORES + lax.rem(core + flip, CORES)

    def hop(axis, d, flip):
        n, e = place(0, d, flip) if axis == X else place(d, 0, flip)
        return (data, n, e)

    def first_slot(offset, slot):
        n, e = place(*offset)
        return (n * (chips * CORES) + e) * cap + slot

    def remote(src, dst, s, r, to):
        return pltpu.make_async_remote_copy(src, dst, s, r, device_id=to, device_id_type=MESH)

    def relay(m):
        ks = plan.pieces_of(m)
        part = pl.ds(ks[0] * half, len(ks) * half)
        a, d, c = plan.msgs[m]
        return remote(send.at[pl.ds(plan.piece_base + ks[0] * half, len(ks) * half)], stage.at[part], s_rel.at[m], r_rel.at[m], hop(a, d, c))

    def forward(k):
        m, q = plan.pieces[k]
        return remote(stage.at[pl.ds(k * half, half)], recv.at[plan.piece_rows(k)], s_fwd.at[k], r_fwd.at[k], hop(1 - plan.msgs[m][0], q, 0))

    def direct(m, src, dst, s, r, sign):
        if m < 0:
            part, to = pl.ds(cap, cap), hop(X, 0, 1)
        else:
            a, d, c = plan.msgs[m]
            part, to = plan.direct_rows(m), hop(a, sign * d, c)
        return remote(src.at[part], dst.at[part], s.at[m + 1], r.at[m + 1], to)

    def out_direct(m):
        return direct(m, send, recv, s_dir, r_dir, 1)

    def back_direct(m):
        return direct(m, y, ret, s_rdir, r_rdir, -1)

    def back_piece(k):
        a, d, c = plan.msgs[plan.pieces[k][0]]
        return remote(y.at[plan.piece_rows(k)], stage2.at[pl.ds(k * half, half)], s_rpc.at[k], r_rpc.at[k], hop(a, -d, c))

    def back_forward(k):
        m, q = plan.pieces[k]
        return remote(stage2.at[pl.ds(k * half, half)], ret.at[plan.piece_rows(k)], s_rfw.at[k], r_rfw.at[k], hop(1 - plan.msgs[m][0], -q, 0))

    tok_copy = pltpu.make_async_copy(tok_hbm, tok, tok_sem)
    tok_copy.start()
    w_copies = [pltpu.make_async_copy(h.at[0], v, w_sem.at[i]) for i, (h, v) in enumerate(((wg_hbm, wg), (wu_hbm, wu), (wd_hbm, wd)))]
    for c in w_copies:
        c.start()
    barrier = pltpu.get_barrier_semaphore()
    near = [(X, 0, 1)] + plan.msgs
    for a, d, c in near:
        pl.semaphore_signal(barrier, inc=1, device_id=hop(a, d, c), device_id_type=MESH)

    ids, slots = ids_ref[...], slots_ref[...]
    pos = jnp.where(slots >= 0, ids * cap + slots, -1)
    spans = plan.spans()

    def pick(lo, hi):
        parts = [s for s in spans if lo <= s[0] < hi]
        hot = [jnp.where(pos - first_slot(off, slot) == lax.broadcasted_iota(jnp.int32, (size, rows), 0), 1.0, 0.0).astype(jnp.bfloat16)
               for _, size, off, slot in parts]
        got = jnp.dot(jnp.concatenate(hot, axis=0), tok[...], preferred_element_type=jnp.float32).astype(jnp.bfloat16)
        if lo == 0:
            recv[pl.ds(0, cap)] = got[:cap]
        send[pl.ds(lo, hi - lo)] = got

    tok_copy.wait()
    step = plan.piece_base, (plan.rows - plan.piece_base) // 4
    for i in range(4):
        pick(step[0] + i * step[1], step[0] + (i + 1) * step[1])
    pl.semaphore_wait(barrier, len(near))
    for m in range(n_msgs):
        relay(m).start()
    for lo in range(0, plan.piece_base, GROUP_ROWS):
        pick(lo, min(lo + GROUP_ROWS, plan.piece_base))
    for m in range(-1, n_msgs):
        out_direct(m).start()

    for b in range(rows // LANES):
        pos_b[pl.ds(b * LANES, LANES), :] = jnp.transpose(jnp.broadcast_to(pos[:, b * LANES:(b + 1) * LANES], (LANES, LANES)))

    for m in range(n_msgs):
        relay(m).wait_recv()
        for k in plan.pieces_of(m):
            forward(k).start()
    for c in w_copies:
        c.wait()

    n_groups = plan.rows // GROUP_ROWS

    def in_group(g):
        lo, hi = g * GROUP_ROWS, (g + 1) * GROUP_ROWS
        ms = [m for m in range(-1, n_msgs) if lo <= (2 + m) * cap < hi]
        ks = [k for k in range(n_pieces) if lo <= plan.piece_base + k * half < hi]
        return ms, ks

    def expert_group(g, carry):
        for j in range(n_groups):
            @pl.when(g == j)
            def _(j=j):
                ms, ks = in_group(j)
                for m in ms:
                    out_direct(m).wait_recv()
                for k in ks:
                    forward(k).wait_recv()
        at = pl.ds(pl.multiple_of(g * GROUP_ROWS, GROUP_ROWS), GROUP_ROWS)
        a = jnp.dot(recv[at], wg[...], preferred_element_type=jnp.float32)
        b = jnp.dot(recv[at], wu[...], preferred_element_type=jnp.float32)
        hid[...] = (jax.nn.silu(a) * b).astype(jnp.bfloat16)
        y[at] = jnp.dot(hid[...], wd[...], preferred_element_type=jnp.float32).astype(jnp.bfloat16)
        for j in range(n_groups):
            @pl.when(g == j)
            def _(j=j):
                ms, ks = in_group(j)
                for m in ms:
                    back_direct(m).start()
                for k in ks:
                    back_piece(k).start()
        return carry

    lax.fori_loop(0, n_groups, expert_group, 0)
    ret[pl.ds(0, cap)] = y[pl.ds(0, cap)]

    lane = lax.broadcasted_iota(jnp.int32, (1, LANES), 1)

    def picked(lo, hi):
        hots = []
        for at in range(lo, hi, LANES):
            want = None
            for first, size, off, slot in spans:
                if at <= first < at + LANES:
                    here = lane - (first - at) + first_slot(off, slot)
                    want = here if want is None else jnp.where(lane >= first - at, here, want)
            hots.append(jnp.where(pos_b[...] == want, 1.0, 0.0).astype(jnp.bfloat16))
        hot = jnp.concatenate(hots, axis=1) if len(hots) > 1 else hots[0]
        return jnp.dot(hot, ret[pl.ds(lo, hi - lo)], preferred_element_type=jnp.float32)

    split = n_pieces // 3
    for k in range(split):
        back_piece(k).wait_recv()
        back_forward(k).start()
    for m in range(-1, n_msgs):
        back_direct(m).wait_recv()
    acc[...] = picked(0, plan.piece_base)
    for k in range(split, n_pieces):
        back_piece(k).wait_recv()
        back_forward(k).start()
    cuts = [0, 16, 28, 32, n_pieces]
    for lo, hi in zip(cuts, cuts[1:]):
        for k in range(lo, hi):
            back_forward(k).wait_recv()
        part = picked(plan.piece_base + lo * half, plan.piece_base + hi * half)
        if hi < n_pieces:
            acc[...] += part
        else:
            out_ref[...] = (acc[...] + part).astype(out_ref.dtype)

    for m in range(n_msgs):
        relay(m).wait_send()
    for m in range(-1, n_msgs):
        out_direct(m).wait_send()
        back_direct(m).wait_send()
    for k in range(n_pieces):
        forward(k).wait_send()
        back_piece(k).wait_send()
        back_forward(k).wait_send()


def solution(mesh):
    nodes, chips = mesh.shape["node"], mesh.shape["expert"] // CORES
    tok_spec = P(("data", "node", "expert"), None)
    weight_spec = P(("node", "expert"), None, None)

    def local_layer(tokens, expert_ids, gate_weights, slot_ids, w_gate, w_up, w_down):
        rows, width = tokens.shape
        ff = w_gate.shape[2]
        cap = capacity(rows, expert_ids.shape[1], nodes * chips * CORES * w_gate.shape[0])
        plan = Plan(nodes, chips, cap)
        n_msgs, n_pieces = len(plan.msgs), len(plan.pieces)
        vmem, hbm = pl.BlockSpec(memory_space=pltpu.VMEM), pl.BlockSpec(memory_space=pl.ANY)
        bf16 = jnp.bfloat16
        sem = lambda n: pltpu.SemaphoreType.DMA((n,))
        picked = pl.pallas_call(
            functools.partial(kernel, plan),
            out_shape=jax.ShapeDtypeStruct((rows, width), bf16),
            in_specs=[vmem, vmem, hbm, hbm, hbm, hbm],
            out_specs=vmem,
            scratch_shapes=[
                pltpu.VMEM((rows, width), bf16),
                pltpu.VMEM((width, ff), bf16),
                pltpu.VMEM((width, ff), bf16),
                pltpu.VMEM((ff, width), bf16),
                pltpu.VMEM((plan.rows, width), bf16),
                pltpu.VMEM((n_pieces * plan.half, width), bf16),
                pltpu.VMEM((plan.rows, width), bf16),
                pltpu.VMEM((GROUP_ROWS, ff), bf16),
                pltpu.VMEM((plan.rows, width), bf16),
                pltpu.VMEM((n_pieces * plan.half, width), bf16),
                pltpu.VMEM((plan.rows, width), bf16),
                pltpu.VMEM((rows, width), jnp.float32),
                pltpu.VMEM((rows, LANES), jnp.int32),
                pltpu.SemaphoreType.DMA,
                sem(3), sem(n_msgs), sem(n_msgs), sem(n_msgs + 1), sem(n_msgs + 1), sem(n_pieces), sem(n_pieces),
                sem(n_msgs + 1), sem(n_msgs + 1), sem(n_pieces), sem(n_pieces), sem(n_pieces), sem(n_pieces),
            ],
            compiler_params=pltpu.CompilerParams(collective_id=0, has_side_effects=True, vmem_limit_bytes=60 * 1024 * 1024),
            name="moe_exchange",
        )(expert_ids.reshape(1, rows), slot_ids.reshape(1, rows), tokens, w_gate, w_up, w_down)
        return (gate_weights * picked.astype(jnp.float32)).astype(bf16)

    return jax.shard_map(local_layer, mesh=mesh, in_specs=(tok_spec, tok_spec, tok_spec, tok_spec, weight_spec, weight_spec, weight_spec), out_specs=tok_spec, check_vma=False)
```

time: 164 us -> 88.6 us (0.54)
  Pallas kernels: 0 us -> 85.4 us
  blocking collectives: 47.9 us -> 0 us
  matrix products: 41.6 us -> 0 us
  waiting for transfers between devices: 41.6 us -> 0 us
  local copies, waits for them, and re-layouts: 22.3 us -> 0.01 us
  starting transfers between devices: 5.18 us -> 0 us
  other arithmetic: 4.57 us -> 2.87 us
    pallas_call x0 -> x1, Pallas kernels: none -> 85.4 us  [local_layer(): pl.pallas_call(functools.partial(kernel, plan), out_shape=jax.ShapeDtypeS...]
    all_to_all x1 -> x0, blocking collectives: 47.9 us -> none  [local_layer(): recv_buf = lax.all_to_all(send_buf, group_axes, 0, 2, tiled=True)]
    dot_general x2 -> x0, matrix products: 41.6 us -> none  [the longest x1 28.4 us: local_layer(): jnp.einsum('erf,efd->erd', hidden, w_down, preferred_element_type=jnp.flo...]
    all_to_all x1 -> x0, waiting for transfers between devices: 41.6 us -> none  [local_layer(): returned = lax.all_to_all(expert_out, group_axes, 1, 0, tiled=True)]
    gather x2 -> x0, local copies, waits for them, and re-layouts: 16.2 us -> none  [the longest x1 9.42 us: local_layer(): send_buf = jnp.take(tokens, src_table, axis=0, mode='fill', fill_value=0)]
    all_to_all x1 -> x0, starting transfers between devices: 5.18 us -> none  [local_layer(): returned = lax.all_to_all(expert_out, group_axes, 1, 0, tiled=True)]
    scatter x1 -> x0, local copies, waits for them, and re-layouts: 4.32 us -> none  [local_layer(): jnp.full((experts * slot_count,), rows, jnp.int32).at[flat_pos.reshape(-1)]]
    select_n x1 -> x0, other arithmetic: 2.11 us -> none  [local_layer(): send_buf = jnp.take(tokens, src_table, axis=0, mode='fill', fill_value=0)]
  transfers between devices with their start and end apart: 1 -> 0, of which waited for: 1 -> 0; matrix products, arithmetic and copies ran while one was open for 0% -> 0% of each run, Pallas kernels for 0% -> 0%
where the time goes in v2:
time: 88.6 us; the launch traced here: 88.2 us
  Pallas kernels  85.4 us (96%)
  other arithmetic  2.87 us (3%)
    pallas_call x1, Pallas kernels, local_layer(): pl.pallas_call(functools.partial(kernel, plan), out_shape=jax.ShapeDtypeS...  85.4 us
    convert_element_type x1, other arithmetic, local_layer(): return (gate_weights * picked.astype(jnp.float32)).astype(bf16)  2.87 us

profile of v2, /device:TPU:96, one launch (start us, length us, event | category | flops | bytes accessed | tf_op | source)
XLA Modules:
  0.0 88.2 jit_solution(13362947262349435524)
XLA Ops:
  0.0 0.0 copy-start
  0.0 85.4 %moe_exchange.1 = bf16[1024,768]{1,0:T(8,128)(2,1)} custom-call(s32[1,1024]{1,0:T(1,128)} %bitcast.4, s32[1,1024]{1,0:T(1,128)} %bitcast.5, bf16[1024,768]{1,0:T(8,128)(2,1)} %tok_hbm.1, bf16[1,768,3072]{2,1,0:T(8,128)(2,1)} %wg_hbm.1, bf16[1,768,3072]{2,1,0:T(8,128)(2,1)} %wu_hbm.1, bf16[1,3072,768]{2,1,0:T(8,128)(2,1)} %wd_hbm.1), custom_call_target="tpu_custom_call" | custom-call | tf_op jit(solution)/shard_map/moe_exchange/pallas_call | solution.py:251
  85.4 0.0 copy-done
  85.4 2.9 %multiply_convert_fusion = bf16[1024,768]{1,0:T(8,128)(2,1)} fusion(bf16[1024,768]{1,0:T(8,128)(2,1)} %moe_exchange.1, f32[1024]{0:T(1024)S(1)} %bitcast.3), kind=kLoop, calls=%fused_computation | loop fusion | flops 2359296 | bytes 3149824 | tf_op jit(solution)/shard_map/convert_element_type | solution.py:277
Async XLA Ops:
  0.0 85.4 %copy-start = (f32[1024,1]{0,1:T(1,128)S(1)}, f32[1024,1]{0,1:T(1,128)}, u32[]{:S(2)}) copy-start(f32[1024,1]{0,1:T(1,128)} %param.9) | copy-start | bytes 12292

commit v3 on v2

--- a/solution.py
+++ b/solution.py
@@ -12,6 +12,8 @@
 CORES = 2
 LANES = 128
 GROUP_ROWS = 256
+PICK_MSGS = 2
+VMEM_MIB = 52
 X, Y = 0, 1
 
 
@@ -52,9 +54,9 @@
         return out
 
 
-def kernel(plan, ids_ref, slots_ref, tok_hbm, wg_hbm, wu_hbm, wd_hbm, out_ref,
-           tok, wg, wu, wd, send, stage, recv, hid, y, stage2, ret, acc, pos_b,
-           tok_sem, w_sem, s_rel, r_rel, s_dir, r_dir, s_fwd, r_fwd, s_rdir, r_rdir, s_rpc, r_rpc, s_rfw, r_rfw):
+def kernel(plan, ids_hbm, slots_hbm, gates_hbm, tok_hbm, wg_hbm, wu_hbm, wd_hbm, acc, hot_ref, last_ref, gate_b,
+           ids_ref, slots_ref, gates_ref, tok, wg, wu, wd, send, stage, recv, hid, y, stage2, ret, pos_b,
+           in_sem, w_sem, s_rel, r_rel, s_dir, r_dir, s_fwd, r_fwd, s_rdir, r_rdir, s_rpc, r_rpc, s_rfw, r_rfw):
     rows = tok.shape[0]
     cap, half = plan.cap, plan.half
     nodes, chips = plan.size[Y], plan.size[X]
@@ -109,16 +111,20 @@
         m, q = plan.pieces[k]
         return remote(stage2.at[pl.ds(k * half, half)], ret.at[plan.piece_rows(k)], s_rfw.at[k], r_rfw.at[k], hop(1 - plan.msgs[m][0], -q, 0))
 
-    tok_copy = pltpu.make_async_copy(tok_hbm, tok, tok_sem)
-    tok_copy.start()
-    w_copies = [pltpu.make_async_copy(h.at[0], v, w_sem.at[i]) for i, (h, v) in enumerate(((wg_hbm, wg), (wu_hbm, wu), (wd_hbm, wd)))]
-    for c in w_copies:
-        c.start()
     barrier = pltpu.get_barrier_semaphore()
     near = [(X, 0, 1)] + plan.msgs
     for a, d, c in near:
         pl.semaphore_signal(barrier, inc=1, device_id=hop(a, d, c), device_id_type=MESH)
-
+    in_copies = [pltpu.make_async_copy(h, v, in_sem.at[i])
+                 for i, (h, v) in enumerate(((ids_hbm, ids_ref), (slots_hbm, slots_ref), (tok_hbm, tok), (gates_hbm, gates_ref)))]
+    for c in in_copies:
+        c.start()
+    w_copies = [pltpu.make_async_copy(h.at[0], v, w_sem.at[i]) for i, (h, v) in enumerate(((wg_hbm, wg), (wu_hbm, wu), (wd_hbm, wd)))]
+
+    for c in in_copies:
+        c.wait()
+    for c in w_copies:
+        c.start()
     ids, slots = ids_ref[...], slots_ref[...]
     pos = jnp.where(slots >= 0, ids * cap + slots, -1)
     spans = plan.spans()
@@ -132,20 +138,27 @@
             recv[pl.ds(0, cap)] = got[:cap]
         send[pl.ds(lo, hi - lo)] = got
 
-    tok_copy.wait()
-    step = plan.piece_base, (plan.rows - plan.piece_base) // 4
-    for i in range(4):
-        pick(step[0] + i * step[1], step[0] + (i + 1) * step[1])
-    pl.semaphore_wait(barrier, len(near))
-    for m in range(n_msgs):
-        relay(m).start()
+    todo = []
+    for m in range(0, n_msgs, PICK_MSGS):
+        ms = list(range(m, min(m + PICK_MSGS, n_msgs)))
+        ks = [k for mm in ms for k in plan.pieces_of(mm)]
+        todo.append((plan.piece_base + ks[0] * half, plan.piece_base + (ks[-1] + 1) * half, [relay(mm) for mm in ms]))
     for lo in range(0, plan.piece_base, GROUP_ROWS):
-        pick(lo, min(lo + GROUP_ROWS, plan.piece_base))
-    for m in range(-1, n_msgs):
-        out_direct(m).start()
+        hi = min(lo + GROUP_ROWS, plan.piece_base)
+        todo.append((lo, hi, [out_direct(m) for m in range(-1, n_msgs) if lo <= (2 + m) * cap < hi]))
+    for i, (lo, hi, _) in enumerate(todo):
+        pick(lo, hi)
+        if i == 1:
+            pl.semaphore_wait(barrier, len(near))
+        if i >= 1:
+            for c in todo[i - 1][2]:
+                c.start()
+    for c in todo[-1][2]:
+        c.start()
 
     for b in range(rows // LANES):
         pos_b[pl.ds(b * LANES, LANES), :] = jnp.transpose(jnp.broadcast_to(pos[:, b * LANES:(b + 1) * LANES], (LANES, LANES)))
+        gate_b[pl.ds(b * LANES, LANES), :] = jnp.transpose(jnp.broadcast_to(gates_ref[:, b * LANES:(b + 1) * LANES], (LANES, LANES)))
 
     for m in range(n_msgs):
         relay(m).wait_recv()
@@ -191,7 +204,7 @@
 
     lane = lax.broadcasted_iota(jnp.int32, (1, LANES), 1)
 
-    def picked(lo, hi):
+    def hot_rows(lo, hi):
         hots = []
         for at in range(lo, hi, LANES):
             want = None
@@ -200,8 +213,10 @@
                     here = lane - (first - at) + first_slot(off, slot)
                     want = here if want is None else jnp.where(lane >= first - at, here, want)
             hots.append(jnp.where(pos_b[...] == want, 1.0, 0.0).astype(jnp.bfloat16))
-        hot = jnp.concatenate(hots, axis=1) if len(hots) > 1 else hots[0]
-        return jnp.dot(hot, ret[pl.ds(lo, hi - lo)], preferred_element_type=jnp.float32)
+        return jnp.concatenate(hots, axis=1) if len(hots) > 1 else hots[0]
+
+    def picked(lo, hi):
+        return jnp.dot(hot_rows(lo, hi), ret[pl.ds(lo, hi - lo)], preferred_element_type=jnp.float32)
 
     split = n_pieces // 3
     for k in range(split):
@@ -213,15 +228,19 @@
     for k in range(split, n_pieces):
         back_piece(k).wait_recv()
         back_forward(k).start()
-    cuts = [0, 16, 28, 32, n_pieces]
-    for lo, hi in zip(cuts, cuts[1:]):
-        for k in range(lo, hi):
+    last = plan.rows - LANES
+    hot_ref[...] = hot_rows(last, plan.rows)
+    lo = plan.piece_base
+    for hi in (lo + n_pieces // 2 // 4 * 4 * half, last):
+        for k in range(n_pieces):
+            if lo <= plan.piece_base + k * half < hi:
+                back_forward(k).wait_recv()
+        acc[...] += picked(lo, hi)
+        lo = hi
+    for k in range(n_pieces):
+        if plan.piece_base + k * half >= last:
             back_forward(k).wait_recv()
-        part = picked(plan.piece_base + lo * half, plan.piece_base + hi * half)
-        if hi < n_pieces:
-            acc[...] += part
-        else:
-            out_ref[...] = (acc[...] + part).astype(out_ref.dtype)
+    last_ref[...] = ret[pl.ds(last, LANES)]
 
     for m in range(n_msgs):
         relay(m).wait_send()
@@ -234,6 +253,21 @@
         back_forward(k).wait_send()
 
 
+def finish(acc, hot, last, gate, out_hbm, buf, sem):
+    rows, width = acc.shape
+    step = rows // 4
+    copies = []
+    for i in range(4):
+        at = pl.ds(i * step, step)
+        total = acc[at] + jnp.dot(hot[at], last[...], preferred_element_type=jnp.float32)
+        for j in range(width // LANES):
+            buf[at, j * LANES:(j + 1) * LANES] = (gate[at] * total[:, j * LANES:(j + 1) * LANES]).astype(buf.dtype)
+        copies.append(pltpu.make_async_copy(buf.at[at], out_hbm.at[at], sem.at[i]))
+        copies[-1].start()
+    for c in copies:
+        c.wait()
+
+
 def solution(mesh):
     nodes, chips = mesh.shape["node"], mesh.shape["expert"] // CORES
     tok_spec = P(("data", "node", "expert"), None)
@@ -248,12 +282,16 @@
         vmem, hbm = pl.BlockSpec(memory_space=pltpu.VMEM), pl.BlockSpec(memory_space=pl.ANY)
         bf16 = jnp.bfloat16
         sem = lambda n: pltpu.SemaphoreType.DMA((n,))
-        picked = pl.pallas_call(
+        parts = pl.pallas_call(
             functools.partial(kernel, plan),
-            out_shape=jax.ShapeDtypeStruct((rows, width), bf16),
-            in_specs=[vmem, vmem, hbm, hbm, hbm, hbm],
-            out_specs=vmem,
+            out_shape=[pltpu.VMEM((rows, width), jnp.float32), pltpu.VMEM((rows, LANES), bf16), pltpu.VMEM((LANES, width), bf16),
+                       pltpu.VMEM((rows, LANES), jnp.float32)],
+            in_specs=[hbm] * 7,
+            out_specs=[vmem] * 4,
             scratch_shapes=[
+                pltpu.VMEM((1, rows), jnp.int32),
+                pltpu.VMEM((1, rows), jnp.int32),
+                pltpu.VMEM((1, rows), jnp.float32),
                 pltpu.VMEM((rows, width), bf16),
                 pltpu.VMEM((width, ff), bf16),
                 pltpu.VMEM((width, ff), bf16),
@@ -265,15 +303,21 @@
                 pltpu.VMEM((plan.rows, width), bf16),
                 pltpu.VMEM((n_pieces * plan.half, width), bf16),
                 pltpu.VMEM((plan.rows, width), bf16),
-                pltpu.VMEM((rows, width), jnp.float32),
                 pltpu.VMEM((rows, LANES), jnp.int32),
-                pltpu.SemaphoreType.DMA,
-                sem(3), sem(n_msgs), sem(n_msgs), sem(n_msgs + 1), sem(n_msgs + 1), sem(n_pieces), sem(n_pieces),
+                sem(4), sem(3), sem(n_msgs), sem(n_msgs), sem(n_msgs + 1), sem(n_msgs + 1), sem(n_pieces), sem(n_pieces),
                 sem(n_msgs + 1), sem(n_msgs + 1), sem(n_pieces), sem(n_pieces), sem(n_pieces), sem(n_pieces),
             ],
-            compiler_params=pltpu.CompilerParams(collective_id=0, has_side_effects=True, vmem_limit_bytes=60 * 1024 * 1024),
+            compiler_params=pltpu.CompilerParams(collective_id=0, has_side_effects=True, vmem_limit_bytes=VMEM_MIB * 1024 * 1024),
             name="moe_exchange",
-        )(expert_ids.reshape(1, rows), slot_ids.reshape(1, rows), tokens, w_gate, w_up, w_down)
-        return (gate_weights * picked.astype(jnp.float32)).astype(bf16)
+        )(expert_ids.reshape(1, rows), slot_ids.reshape(1, rows), gate_weights.reshape(1, rows), tokens, w_gate, w_up, w_down)
+        return pl.pallas_call(
+            finish,
+            out_shape=jax.ShapeDtypeStruct((rows, width), bf16),
+            in_specs=[vmem] * 4,
+            out_specs=hbm,
+            scratch_shapes=[pltpu.VMEM((rows, width), bf16), sem(4)],
+            compiler_params=pltpu.CompilerParams(vmem_limit_bytes=8 * 1024 * 1024),
+            name="moe_finish",
+        )(*parts)
 
     return jax.shard_map(local_layer, mesh=mesh, in_specs=(tok_spec, tok_spec, tok_spec, tok_spec, weight_spec, weight_spec, weight_spec), out_specs=tok_spec, check_vma=False)

time: 88.6 us -> 80.9 us (0.913)
  Pallas kernels: 85.4 us -> 80.6 us
  other arithmetic: 2.87 us -> 0 us
    pallas_call x1 -> x2, Pallas kernels: 85.4 us -> 80.6 us  [the longest x1 79.1 us: local_layer(): pl.pallas_call(functools.partial(kernel, plan), out_shape=[pltpu.VMEM((ro...]
    convert_element_type x1 -> x0, other arithmetic: 2.87 us -> none  [local_layer(): return (gate_weights * picked.astype(jnp.float32)).astype(bf16)]
where the time goes in v3:
time: 80.9 us; the launch traced here: 80.8 us
  Pallas kernels  80.6 us (100%)
    pallas_call x1, Pallas kernels, local_layer(): pl.pallas_call(functools.partial(kernel, plan), out_shape=[pltpu.VMEM((ro...  79.1 us

profile of v3, /device:TPU:96, one launch (start us, length us, event | category | flops | bytes accessed | tf_op | source)
XLA Modules:
  0.0 80.8 jit_solution(747043767368635997)
XLA Ops:
  0.0 79.1 %moe_exchange.1 = (f32[1024,768]{1,0:T(8,128)S(1)}, bf16[1024,128]{1,0:T(8,128)(2,1)S(1)}, bf16[128,768]{1,0:T(8,128)(2,1)S(1)}, f32[1024,128]{1,0:T(8,128)S(1)}) custom-call(s32[1,1024]{1,0:T(1,128)} %bitcast.3, s32[1,1024]{1,0:T(1,128)} %bitcast.4, f32[1,1024]{1,0:T(1,128)} %bitcast.5, bf16[1024,768]{1,0:T(8,128)(2,1)} %tok_hbm.1, ...), custom_call_target="tpu_custom_call" | custom-call | tf_op jit(solution)/shard_map/moe_exchange/pallas_call | solution.py:285
  79.1 1.5 %moe_finish.1 = bf16[1024,768]{1,0:T(8,128)(2,1)} custom-call(f32[1024,768]{1,0:T(8,128)S(1)} %get-tuple-element.9.acc, bf16[1024,128]{1,0:T(8,128)(2,1)S(1)} %get-tuple-element.10.hot, bf16[128,768]{1,0:T(8,128)(2,1)S(1)} %get-tuple-element.11.last, f32[1024,128]{1,0:T(8,128)S(1)} %get-tuple-element.12.gate), custom_call_target="tpu_custom_call" | custom-call | tf_op jit(solution)/shard_map/moe_finish/pallas_call | solution.py:313

commit v4 on v3

--- a/solution.py
+++ b/solution.py
@@ -56,7 +56,7 @@
 
 def kernel(plan, ids_hbm, slots_hbm, gates_hbm, tok_hbm, wg_hbm, wu_hbm, wd_hbm, acc, hot_ref, last_ref, gate_b,
            ids_ref, slots_ref, gates_ref, tok, wg, wu, wd, send, stage, recv, hid, y, stage2, ret, pos_b,
-           in_sem, w_sem, s_rel, r_rel, s_dir, r_dir, s_fwd, r_fwd, s_rdir, r_rdir, s_rpc, r_rpc, s_rfw, r_rfw):
+           in_sem, w_sem, sent, r_rel, r_grp, r_rdir, r_rpc, r_ret):
     rows = tok.shape[0]
     cap, half = plan.cap, plan.half
     nodes, chips = plan.size[Y], plan.size[X]
@@ -83,11 +83,24 @@
         ks = plan.pieces_of(m)
         part = pl.ds(ks[0] * half, len(ks) * half)
         a, d, c = plan.msgs[m]
-        return remote(send.at[pl.ds(plan.piece_base + ks[0] * half, len(ks) * half)], stage.at[part], s_rel.at[m], r_rel.at[m], hop(a, d, c))
+        return remote(send.at[pl.ds(plan.piece_base + ks[0] * half, len(ks) * half)], stage.at[part], sent.at[0], r_rel.at[m], hop(a, d, c))
 
     def forward(k):
         m, q = plan.pieces[k]
-        return remote(stage.at[pl.ds(k * half, half)], recv.at[plan.piece_rows(k)], s_fwd.at[k], r_fwd.at[k], hop(1 - plan.msgs[m][0], q, 0))
+        return remote(stage.at[pl.ds(k * half, half)], recv.at[plan.piece_rows(k)], sent.at[1], r_grp.at[group_of(plan.piece_base + k * half)], hop(1 - plan.msgs[m][0], q, 0))
+
+    last = plan.rows - LANES
+    cut = plan.piece_base + (n_pieces // 2 // 4 * 4) * half
+
+    def ret_part(row):
+        return 0 if row < cut else 1 if row < last else 2
+
+    def arrived(ref, lo, hi, sem):
+        part = ref.at[pl.ds(lo, hi - lo)]
+        pltpu.make_async_copy(part, part, sem).wait()
+
+    def group_of(row):
+        return row // GROUP_ROWS
 
     def direct(m, src, dst, s, r, sign):
         if m < 0:
@@ -95,21 +108,21 @@
         else:
             a, d, c = plan.msgs[m]
             part, to = plan.direct_rows(m), hop(a, sign * d, c)
-        return remote(src.at[part], dst.at[part], s.at[m + 1], r.at[m + 1], to)
+        return remote(src.at[part], dst.at[part], s, r, to)
 
     def out_direct(m):
-        return direct(m, send, recv, s_dir, r_dir, 1)
+        return direct(m, send, recv, sent.at[2], r_grp.at[group_of((2 + m) * cap)], 1)
 
     def back_direct(m):
-        return direct(m, y, ret, s_rdir, r_rdir, -1)
+        return direct(m, y, ret, sent.at[3], r_rdir, -1)
 
     def back_piece(k):
         a, d, c = plan.msgs[plan.pieces[k][0]]
-        return remote(y.at[plan.piece_rows(k)], stage2.at[pl.ds(k * half, half)], s_rpc.at[k], r_rpc.at[k], hop(a, -d, c))
+        return remote(y.at[plan.piece_rows(k)], stage2.at[pl.ds(k * half, half)], sent.at[4], r_rpc.at[plan.pieces[k][0]], hop(a, -d, c))
 
     def back_forward(k):
         m, q = plan.pieces[k]
-        return remote(stage2.at[pl.ds(k * half, half)], ret.at[plan.piece_rows(k)], s_rfw.at[k], r_rfw.at[k], hop(1 - plan.msgs[m][0], -q, 0))
+        return remote(stage2.at[pl.ds(k * half, half)], ret.at[plan.piece_rows(k)], sent.at[5], r_ret.at[ret_part(plan.piece_base + k * half)], hop(1 - plan.msgs[m][0], -q, 0))
 
     barrier = pltpu.get_barrier_semaphore()
     near = [(X, 0, 1)] + plan.msgs
@@ -179,11 +192,7 @@
         for j in range(n_groups):
             @pl.when(g == j)
             def _(j=j):
-                ms, ks = in_group(j)
-                for m in ms:
-                    out_direct(m).wait_recv()
-                for k in ks:
-                    forward(k).wait_recv()
+                arrived(recv, max(j * GROUP_ROWS, cap), (j + 1) * GROUP_ROWS, r_grp.at[j])
         at = pl.ds(pl.multiple_of(g * GROUP_ROWS, GROUP_ROWS), GROUP_ROWS)
         a = jnp.dot(recv[at], wg[...], preferred_element_type=jnp.float32)
         b = jnp.dot(recv[at], wu[...], preferred_element_type=jnp.float32)
@@ -218,39 +227,27 @@
     def picked(lo, hi):
         return jnp.dot(hot_rows(lo, hi), ret[pl.ds(lo, hi - lo)], preferred_element_type=jnp.float32)
 
-    split = n_pieces // 3
-    for k in range(split):
-        back_piece(k).wait_recv()
-        back_forward(k).start()
-    for m in range(-1, n_msgs):
-        back_direct(m).wait_recv()
+    def send_back(ms):
+        for m in ms:
+            ks = plan.pieces_of(m)
+            arrived(stage2, ks[0] * half, (ks[-1] + 1) * half, r_rpc.at[m])
+            for k in ks:
+                back_forward(k).start()
+
+    send_back(range(n_msgs // 3))
+    arrived(ret, cap, plan.piece_base, r_rdir)
     acc[...] = picked(0, plan.piece_base)
-    for k in range(split, n_pieces):
-        back_piece(k).wait_recv()
-        back_forward(k).start()
-    last = plan.rows - LANES
+    send_back(range(n_msgs // 3, n_msgs))
     hot_ref[...] = hot_rows(last, plan.rows)
-    lo = plan.piece_base
-    for hi in (lo + n_pieces // 2 // 4 * 4 * half, last):
-        for k in range(n_pieces):
-            if lo <= plan.piece_base + k * half < hi:
-                back_forward(k).wait_recv()
+    for lo, hi in ((plan.piece_base, cut), (cut, last)):
+        arrived(ret, lo, hi, r_ret.at[ret_part(lo)])
         acc[...] += picked(lo, hi)
-        lo = hi
-    for k in range(n_pieces):
-        if plan.piece_base + k * half >= last:
-            back_forward(k).wait_recv()
+    arrived(ret, last, plan.rows, r_ret.at[2])
     last_ref[...] = ret[pl.ds(last, LANES)]
 
-    for m in range(n_msgs):
-        relay(m).wait_send()
-    for m in range(-1, n_msgs):
-        out_direct(m).wait_send()
-        back_direct(m).wait_send()
-    for k in range(n_pieces):
-        forward(k).wait_send()
-        back_piece(k).wait_send()
-        back_forward(k).wait_send()
+    n_rows = plan.rows - plan.piece_base
+    for i, (lo, hi) in enumerate(((0, n_rows), (0, n_rows), (cap, plan.piece_base), (cap, plan.piece_base), (0, n_rows), (0, n_rows))):
+        arrived(send, lo, hi, sent.at[i])
 
 
 def finish(acc, hot, last, gate, out_hbm, buf, sem):
@@ -304,8 +301,7 @@
                 pltpu.VMEM((n_pieces * plan.half, width), bf16),
                 pltpu.VMEM((plan.rows, width), bf16),
                 pltpu.VMEM((rows, LANES), jnp.int32),
-                sem(4), sem(3), sem(n_msgs), sem(n_msgs), sem(n_msgs + 1), sem(n_msgs + 1), sem(n_pieces), sem(n_pieces),
-                sem(n_msgs + 1), sem(n_msgs + 1), sem(n_pieces), sem(n_pieces), sem(n_pieces), sem(n_pieces),
+                sem(4), sem(3), sem(6), sem(n_msgs), sem(plan.rows // GROUP_ROWS), pltpu.SemaphoreType.DMA, sem(n_msgs), sem(3),
             ],
             compiler_params=pltpu.CompilerParams(collective_id=0, has_side_effects=True, vmem_limit_bytes=VMEM_MIB * 1024 * 1024),
             name="moe_exchange",

time: 80.9 us -> 78.2 us (0.967)
  Pallas kernels: 80.6 us -> 77.9 us
    pallas_call x1, Pallas kernels: 79.1 us -> 76.5 us  [local_layer(): pl.pallas_call(functools.partial(kernel, plan), out_shape=[pltpu.VMEM((ro...]
where the time goes in v4:
time: 78.2 us; the launch traced here: 78.1 us
  Pallas kernels  77.9 us (100%)
    pallas_call x1, Pallas kernels, local_layer(): pl.pallas_call(functools.partial(kernel, plan), out_shape=[pltpu.VMEM((ro...  76.5 us

profile of v4, /device:TPU:96, one launch (start us, length us, event | category | flops | bytes accessed | tf_op | source)
XLA Modules:
  0.0 78.1 jit_solution(14018449724699607007)
XLA Ops:
  0.0 76.5 %moe_exchange.1 = (f32[1024,768]{1,0:T(8,128)S(1)}, bf16[1024,128]{1,0:T(8,128)(2,1)S(1)}, bf16[128,768]{1,0:T(8,128)(2,1)S(1)}, f32[1024,128]{1,0:T(8,128)S(1)}) custom-call(s32[1,1024]{1,0:T(1,128)} %bitcast.3, s32[1,1024]{1,0:T(1,128)} %bitcast.4, f32[1,1024]{1,0:T(1,128)} %bitcast.5, bf16[1024,768]{1,0:T(8,128)(2,1)} %tok_hbm.1, ...), custom_call_target="tpu_custom_call" | custom-call | tf_op jit(solution)/shard_map/moe_exchange/pallas_call | solution.py:282
  76.5 1.5 %moe_finish.1 = bf16[1024,768]{1,0:T(8,128)(2,1)} custom-call(f32[1024,768]{1,0:T(8,128)S(1)} %get-tuple-element.9.acc, bf16[1024,128]{1,0:T(8,128)(2,1)S(1)} %get-tuple-element.10.hot, bf16[128,768]{1,0:T(8,128)(2,1)S(1)} %get-tuple-element.11.last, f32[1024,128]{1,0:T(8,128)S(1)} %get-tuple-element.12.gate), custom_call_target="tpu_custom_call" | custom-call | tf_op jit(solution)/shard_map/moe_finish/pallas_call | solution.py:309

commit v5 on v4

--- a/solution.py
+++ b/solution.py
@@ -14,6 +14,7 @@
 GROUP_ROWS = 256
 PICK_MSGS = 2
 VMEM_MIB = 52
+OUT_CHUNKS = 8
 X, Y = 0, 1
 
 
@@ -83,7 +84,7 @@
         ks = plan.pieces_of(m)
         part = pl.ds(ks[0] * half, len(ks) * half)
         a, d, c = plan.msgs[m]
-        return remote(send.at[pl.ds(plan.piece_base + ks[0] * half, len(ks) * half)], stage.at[part], sent.at[0], r_rel.at[m], hop(a, d, c))
+        return remote(send.at[pl.ds(plan.piece_base + ks[0] * half, len(ks) * half)], stage.at[part], sent.at[0], r_rel.at[m // 2], hop(a, d, c))
 
     def forward(k):
         m, q = plan.pieces[k]
@@ -91,6 +92,11 @@
 
     last = plan.rows - LANES
     cut = plan.piece_base + (n_pieces // 2 // 4 * 4) * half
+
+    batches = [range(0, n_msgs // 2), range(n_msgs // 2, n_msgs - 3)] + [range(m, m + 1) for m in range(n_msgs - 3, n_msgs)]
+
+    def batch_of(m):
+        return next(i for i, b in enumerate(batches) if m in b)
 
     def ret_part(row):
         return 0 if row < cut else 1 if row < last else 2
@@ -118,7 +124,7 @@
 
     def back_piece(k):
         a, d, c = plan.msgs[plan.pieces[k][0]]
-        return remote(y.at[plan.piece_rows(k)], stage2.at[pl.ds(k * half, half)], sent.at[4], r_rpc.at[plan.pieces[k][0]], hop(a, -d, c))
+        return remote(y.at[plan.piece_rows(k)], stage2.at[pl.ds(k * half, half)], sent.at[4], r_rpc.at[batch_of(plan.pieces[k][0])], hop(a, -d, c))
 
     def back_forward(k):
         m, q = plan.pieces[k]
@@ -173,9 +179,10 @@
         pos_b[pl.ds(b * LANES, LANES), :] = jnp.transpose(jnp.broadcast_to(pos[:, b * LANES:(b + 1) * LANES], (LANES, LANES)))
         gate_b[pl.ds(b * LANES, LANES), :] = jnp.transpose(jnp.broadcast_to(gates_ref[:, b * LANES:(b + 1) * LANES], (LANES, LANES)))
 
-    for m in range(n_msgs):
-        relay(m).wait_recv()
-        for k in plan.pieces_of(m):
+    for i in range(n_msgs // 2):
+        ks = plan.pieces_of(2 * i) + plan.pieces_of(2 * i + 1)
+        arrived(stage, ks[0] * half, (ks[-1] + 1) * half, r_rel.at[i])
+        for k in ks:
             forward(k).start()
     for c in w_copies:
         c.wait()
@@ -197,7 +204,8 @@
         a = jnp.dot(recv[at], wg[...], preferred_element_type=jnp.float32)
         b = jnp.dot(recv[at], wu[...], preferred_element_type=jnp.float32)
         hid[...] = (jax.nn.silu(a) * b).astype(jnp.bfloat16)
-        y[at] = jnp.dot(hid[...], wd[...], preferred_element_type=jnp.float32).astype(jnp.bfloat16)
+        rounded = jnp.dot(hid[...], wd[...], preferred_element_type=jnp.float32).astype(jnp.bfloat16).astype(jnp.float32)
+        y[at] = jnp.where(jnp.abs(rounded) < jnp.inf, rounded, 0.0).astype(jnp.bfloat16)
         for j in range(n_groups):
             @pl.when(g == j)
             def _(j=j):
@@ -227,17 +235,17 @@
     def picked(lo, hi):
         return jnp.dot(hot_rows(lo, hi), ret[pl.ds(lo, hi - lo)], preferred_element_type=jnp.float32)
 
-    def send_back(ms):
-        for m in ms:
-            ks = plan.pieces_of(m)
-            arrived(stage2, ks[0] * half, (ks[-1] + 1) * half, r_rpc.at[m])
+    def send_back(ids):
+        for i in ids:
+            ks = [k for m in batches[i] for k in plan.pieces_of(m)]
+            arrived(stage2, ks[0] * half, (ks[-1] + 1) * half, r_rpc.at[i])
             for k in ks:
                 back_forward(k).start()
 
-    send_back(range(n_msgs // 3))
+    send_back([0])
     arrived(ret, cap, plan.piece_base, r_rdir)
     acc[...] = picked(0, plan.piece_base)
-    send_back(range(n_msgs // 3, n_msgs))
+    send_back(range(1, len(batches)))
     hot_ref[...] = hot_rows(last, plan.rows)
     for lo, hi in ((plan.piece_base, cut), (cut, last)):
         arrived(ret, lo, hi, r_ret.at[ret_part(lo)])
@@ -252,17 +260,14 @@
 
 def finish(acc, hot, last, gate, out_hbm, buf, sem):
     rows, width = acc.shape
-    step = rows // 4
-    copies = []
-    for i in range(4):
+    step = rows // OUT_CHUNKS
+    for i in range(OUT_CHUNKS):
         at = pl.ds(i * step, step)
         total = acc[at] + jnp.dot(hot[at], last[...], preferred_element_type=jnp.float32)
         for j in range(width // LANES):
             buf[at, j * LANES:(j + 1) * LANES] = (gate[at] * total[:, j * LANES:(j + 1) * LANES]).astype(buf.dtype)
-        copies.append(pltpu.make_async_copy(buf.at[at], out_hbm.at[at], sem.at[i]))
-        copies[-1].start()
-    for c in copies:
-        c.wait()
+        pltpu.make_async_copy(buf.at[at], out_hbm.at[at], sem).start()
+    pltpu.make_async_copy(buf, out_hbm, sem).wait()
 
 
 def solution(mesh):
@@ -301,7 +306,7 @@
                 pltpu.VMEM((n_pieces * plan.half, width), bf16),
                 pltpu.VMEM((plan.rows, width), bf16),
                 pltpu.VMEM((rows, LANES), jnp.int32),
-                sem(4), sem(3), sem(6), sem(n_msgs), sem(plan.rows // GROUP_ROWS), pltpu.SemaphoreType.DMA, sem(n_msgs), sem(3),
+                sem(4), sem(3), sem(6), sem(n_msgs // 2), sem(plan.rows // GROUP_ROWS), pltpu.SemaphoreType.DMA, sem(5), sem(3),
             ],
             compiler_params=pltpu.CompilerParams(collective_id=0, has_side_effects=True, vmem_limit_bytes=VMEM_MIB * 1024 * 1024),
             name="moe_exchange",
@@ -311,7 +316,7 @@
             out_shape=jax.ShapeDtypeStruct((rows, width), bf16),
             in_specs=[vmem] * 4,
             out_specs=hbm,
-            scratch_shapes=[pltpu.VMEM((rows, width), bf16), sem(4)],
+            scratch_shapes=[pltpu.VMEM((rows, width), bf16), pltpu.SemaphoreType.DMA],
             compiler_params=pltpu.CompilerParams(vmem_limit_bytes=8 * 1024 * 1024),
             name="moe_finish",
         )(*parts)

time: 78.2 us -> 78 us (level)
  no operation moved by 1% of the time
where the time goes in v5:
time: 78 us; the launch traced here: 77.9 us
  Pallas kernels  77.8 us (100%)
    pallas_call x1, Pallas kernels, local_layer(): pl.pallas_call(functools.partial(kernel, plan), out_shape=[pltpu.VMEM((ro...  76.4 us

profile of v5, /device:TPU:96, one launch (start us, length us, event | category | flops | bytes accessed | tf_op | source)
XLA Modules:
  0.0 77.9 jit_solution(17391772372226096019)
XLA Ops:
  0.0 76.4 %moe_exchange.1 = (f32[1024,768]{1,0:T(8,128)S(1)}, bf16[1024,128]{1,0:T(8,128)(2,1)S(1)}, bf16[128,768]{1,0:T(8,128)(2,1)S(1)}, f32[1024,128]{1,0:T(8,128)S(1)}) custom-call(s32[1,1024]{1,0:T(1,128)} %bitcast.3, s32[1,1024]{1,0:T(1,128)} %bitcast.4, f32[1,1024]{1,0:T(1,128)} %bitcast.5, bf16[1024,768]{1,0:T(8,128)(2,1)} %tok_hbm.1, ...), custom_call_target="tpu_custom_call" | custom-call | tf_op jit(solution)/shard_map/moe_exchange/pallas_call | solution.py:287
  76.4 1.4 %moe_finish.1 = bf16[1024,768]{1,0:T(8,128)(2,1)} custom-call(f32[1024,768]{1,0:T(8,128)S(1)} %get-tuple-element.9.acc, bf16[1024,128]{1,0:T(8,128)(2,1)S(1)} %get-tuple-element.10.hot, bf16[128,768]{1,0:T(8,128)(2,1)S(1)} %get-tuple-element.11.last, f32[1024,128]{1,0:T(8,128)S(1)} %get-tuple-element.12.gate), custom_call_target="tpu_custom_call" | custom-call | tf_op jit(solution)/shard_map/moe_finish/pallas_call | solution.py:314

commit v6 on v5

--- a/solution.py
+++ b/solution.py
@@ -117,21 +117,21 @@
         return remote(src.at[part], dst.at[part], s, r, to)
 
     def out_direct(m):
-        return direct(m, send, recv, sent.at[2], r_grp.at[group_of((2 + m) * cap)], 1)
+        return direct(m, send, recv, sent.at[0], r_grp.at[group_of((2 + m) * cap)], 1)
 
     def back_direct(m):
-        return direct(m, y, ret, sent.at[3], r_rdir, -1)
+        return direct(m, y, ret, sent.at[1], r_rdir, -1)
 
     def back_piece(k):
         a, d, c = plan.msgs[plan.pieces[k][0]]
-        return remote(y.at[plan.piece_rows(k)], stage2.at[pl.ds(k * half, half)], sent.at[4], r_rpc.at[batch_of(plan.pieces[k][0])], hop(a, -d, c))
+        return remote(y.at[plan.piece_rows(k)], stage2.at[pl.ds(k * half, half)], sent.at[2], r_rpc.at[batch_of(plan.pieces[k][0])], hop(a, -d, c))
 
     def back_forward(k):
         m, q = plan.pieces[k]
-        return remote(stage2.at[pl.ds(k * half, half)], ret.at[plan.piece_rows(k)], sent.at[5], r_ret.at[ret_part(plan.piece_base + k * half)], hop(1 - plan.msgs[m][0], -q, 0))
+        return remote(stage2.at[pl.ds(k * half, half)], ret.at[plan.piece_rows(k)], sent.at[3], r_ret.at[ret_part(plan.piece_base + k * half)], hop(1 - plan.msgs[m][0], -q, 0))
 
     barrier = pltpu.get_barrier_semaphore()
-    near = [(X, 0, 1)] + plan.msgs
+    near = sorted(plan.msgs, key=lambda m: -min(m[1], plan.size[m[0]] - m[1])) + [(X, 0, 1)]
     for a, d, c in near:
         pl.semaphore_signal(barrier, inc=1, device_id=hop(a, d, c), device_id_type=MESH)
     in_copies = [pltpu.make_async_copy(h, v, in_sem.at[i])
@@ -254,8 +254,9 @@
     last_ref[...] = ret[pl.ds(last, LANES)]
 
     n_rows = plan.rows - plan.piece_base
-    for i, (lo, hi) in enumerate(((0, n_rows), (0, n_rows), (cap, plan.piece_base), (cap, plan.piece_base), (0, n_rows), (0, n_rows))):
-        arrived(send, lo, hi, sent.at[i])
+    d_rows = plan.piece_base - cap
+    for i, n in enumerate((n_rows + d_rows, n_rows + d_rows, n_rows, n_rows)):
+        arrived(send, 0, n, sent.at[i])
 
 
 def finish(acc, hot, last, gate, out_hbm, buf, sem):
@@ -306,7 +307,7 @@
                 pltpu.VMEM((n_pieces * plan.half, width), bf16),
                 pltpu.VMEM((plan.rows, width), bf16),
                 pltpu.VMEM((rows, LANES), jnp.int32),
-                sem(4), sem(3), sem(6), sem(n_msgs // 2), sem(plan.rows // GROUP_ROWS), pltpu.SemaphoreType.DMA, sem(5), sem(3),
+                sem(4), sem(3), sem(4), sem(n_msgs // 2), sem(plan.rows // GROUP_ROWS), pltpu.SemaphoreType.DMA, sem(5), sem(3),
             ],
             compiler_params=pltpu.CompilerParams(collective_id=0, has_side_effects=True, vmem_limit_bytes=VMEM_MIB * 1024 * 1024),
             name="moe_exchange",

time: 78 us -> 78 us (level)
  no operation moved by 1% of the time
where the time goes in v6:
time: 78 us; the launch traced here: 77.9 us
  Pallas kernels  77.7 us (100%)
    pallas_call x1, Pallas kernels, local_layer(): pl.pallas_call(functools.partial(kernel, plan), out_shape=[pltpu.VMEM((ro...  76.4 us

profile of v6, /device:TPU:96, one launch (start us, length us, event | category | flops | bytes accessed | tf_op | source)
XLA Modules:
  0.0 77.9 jit_solution(1974622383606366863)
XLA Ops:
  0.0 76.4 %moe_exchange.1 = (f32[1024,768]{1,0:T(8,128)S(1)}, bf16[1024,128]{1,0:T(8,128)(2,1)S(1)}, bf16[128,768]{1,0:T(8,128)(2,1)S(1)}, f32[1024,128]{1,0:T(8,128)S(1)}) custom-call(s32[1,1024]{1,0:T(1,128)} %bitcast.3, s32[1,1024]{1,0:T(1,128)} %bitcast.4, f32[1,1024]{1,0:T(1,128)} %bitcast.5, bf16[1024,768]{1,0:T(8,128)(2,1)} %tok_hbm.1, ...), custom_call_target="tpu_custom_call" | custom-call | tf_op jit(solution)/shard_map/moe_exchange/pallas_call | solution.py:288
  76.4 1.4 %moe_finish.1 = bf16[1024,768]{1,0:T(8,128)(2,1)} custom-call(f32[1024,768]{1,0:T(8,128)S(1)} %get-tuple-element.9.acc, bf16[1024,128]{1,0:T(8,128)(2,1)S(1)} %get-tuple-element.10.hot, bf16[128,768]{1,0:T(8,128)(2,1)S(1)} %get-tuple-element.11.last, f32[1024,128]{1,0:T(8,128)S(1)} %get-tuple-element.12.gate), custom_call_target="tpu_custom_call" | custom-call | tf_op jit(solution)/shard_map/moe_finish/pallas_call | solution.py:315
